TPU v7x, 32 devices: a whole 2x2x4 slice. The times are simulated.
32 devices in a mesh: seq: 8 (over z, y), ch: 4 (over x, core).
Axes of the slice: x: 2, y: 2, z: 4, core: 2. Of those that a mesh axis runs over, the one named last changes fastest.
Arguments:
- inputs: bfloat16 [8192, 768], P(('seq', 'ch')), may hold values from -6 to 6
- gain_one: float32 [768], replicated, may hold values from 0.5 to 1.5
- shift_one: float32 [768], replicated, may hold values from -1.5 to 1.5
- conv_weight: bfloat16 [3, 768, 384], P(None, None, 'ch'), may hold values from -0.125 to 0.125
- gain_two: float32 [384], P('ch'), may hold values from 0.5 to 1.5
- shift_two: float32 [384], P('ch'), may hold values from -1.5 to 1.5
- mix_weight: bfloat16 [384, 768], P('ch'), may hold values from -0.3125 to 0.3125
- head_weight: bfloat16 [768, 6956], P('ch'), may hold values from -0.21875 to 0.21875
- head_bias: float32 [6956], replicated, may hold values from -2 to 2
- species: int32 [8], replicated, may hold values from 0 to 1, as said below
- counts: int32 [8192, 5313], P(('seq', 'ch')), may hold values from 0 to 3
Outputs:
- outputs: bfloat16 [8192, 768], P(('seq', 'ch'))
- input_grad: float32 [8192, 768], P(('seq', 'ch'))
- gain_one_grad: float32 [768], replicated
- shift_one_grad: float32 [768], replicated
- conv_weight_grad: float32 [3, 768, 384], P(None, None, 'ch')
- gain_two_grad: float32 [384], P('ch')
- shift_two_grad: float32 [384], P('ch')
- mix_weight_grad: float32 [384, 768], P('ch')
- head_weight_grad: float32 [768, 6956], P(('seq', 'ch'))
- head_bias_grad: float32 [6956], replicated
Inputs may be any that keep to these rules, and one draw needn't show every extreme that they name: Each window holds one species, given by species[w]; both species occur in every draw.
All inputs are finite; a program needn't handle non-finite values.
Results may differ from a plain program's by a relative error of at most 0.014.
Values may be sent and summed in bfloat16 or wider, within the bound.
A program may use at most 192 MiB of HBM per device.

v0:
```python
import jax
import jax.numpy as jnp
from jax import lax
from jax.sharding import PartitionSpec as P

HUMAN = 5313
MOUSE = 1643
DILATION_STEP = 11
TAPS = 3
WINDOW_BINS = 1024
SHIFT = 512


norm_eps = 1e-05
contract_rows = (((0,), (0,)), ((), ()))
contract_cols = (((1,), (1,)), ((), ()))


def with_halo(cells, sides, width):
    for axis, dim in sides:
        count = lax.axis_size(axis)
        head = lax.slice_in_dim(cells, 0, width, axis=dim)
        tail = lax.slice_in_dim(cells, cells.shape[dim] - width, cells.shape[dim], axis=dim)
        cells = jnp.concatenate(
            [
                lax.ppermute(tail, axis, [(i, (i + 1) % count) for i in range(count)]),
                cells,
                lax.ppermute(head, axis, [((i + 1) % count, i) for i in range(count)]),
            ],
            axis=dim,
        )
    return cells


def window_lookup(position, total_bins):
    return jnp.mod(position - SHIFT, total_bins) // WINDOW_BINS


def gelu_grad(value, upstream):
    _, pullback = jax.vjp(jax.nn.gelu, value)
    return pullback(upstream)[0]


def poisson_grad(logits, target):
    rate = jax.nn.softplus(logits)
    return (jax.nn.sigmoid(logits) * (1.0 - target / rate)).astype(jnp.bfloat16)


def on_device(
    inputs,
    gain_one,
    shift_one,
    conv_weight,
    gain_two,
    shift_two,
    mix_weight,
    head_weight,
    head_bias,
    species,
    counts,
):
    seq_count = lax.axis_size("seq")
    ch_count = lax.axis_size("ch")
    seq_index = lax.axis_index("seq")
    ch_index = lax.axis_index("ch")
    local_rows = inputs.shape[0]
    width = inputs.shape[1]
    conv_cols = conv_weight.shape[2]
    residual_rows = local_rows * ch_count
    every_bin_list = residual_rows * seq_count
    inv_bins = 1.0 / every_bin_list
    input_f = inputs.astype(jnp.float32)
    sum_one, square_one = lax.psum(
        (jnp.sum(input_f, 0), jnp.sum(input_f * input_f, 0)), ("seq", "ch")
    )
    mean_one = sum_one * inv_bins
    scale_one = lax.rsqrt(square_one * inv_bins - mean_one * mean_one + norm_eps)
    normed_one = (input_f - mean_one) * scale_one
    pre_one = normed_one * gain_one + shift_one
    act_one = jax.nn.gelu(pre_one).astype(jnp.bfloat16)
    residual_block = lax.all_gather(act_one, "ch", axis=0, tiled=True)
    padded_input = with_halo(residual_block, (("seq", 0),), DILATION_STEP)
    bin_positions = seq_index * residual_rows + jnp.arange(residual_rows, dtype=jnp.int32)
    local_window = window_lookup(bin_positions, every_bin_list)
    fwd_masks = [
        window_lookup(bin_positions + (kernel_tap_index - 1) * DILATION_STEP, every_bin_list)
        == local_window
        for kernel_tap_index in range(TAPS)
    ]
    back_masks = [
        (
            window_lookup(bin_positions - (kernel_tap_index - 1) * DILATION_STEP, every_bin_list)
            == local_window
        ).astype(jnp.float32)[:, None]
        for kernel_tap_index in range(TAPS)
    ]
    conv_out = jnp.zeros((residual_rows, conv_cols), jnp.float32)
    for kernel_tap_index in range(TAPS):
        product = jnp.dot(
            padded_input[
                kernel_tap_index * DILATION_STEP : kernel_tap_index * DILATION_STEP + residual_rows
            ],
            conv_weight[kernel_tap_index],
            preferred_element_type=jnp.float32,
        )
        conv_out = conv_out + jnp.where(fwd_masks[kernel_tap_index][:, None], product, 0.0)
    sum_two, square_two = lax.psum((jnp.sum(conv_out, 0), jnp.sum(conv_out * conv_out, 0)), "seq")
    mean_two = sum_two * inv_bins
    scale_two = lax.rsqrt(square_two * inv_bins - mean_two * mean_two + norm_eps)
    normed_two = (conv_out - mean_two) * scale_two
    pre_two = normed_two * gain_two + shift_two
    act_two = jax.nn.gelu(pre_two).astype(jnp.bfloat16)
    branch = lax.psum_scatter(
        jnp.dot(act_two, mix_weight, preferred_element_type=jnp.float32).astype(jnp.bfloat16),
        "ch",
        scatter_dimension=0,
        tiled=True,
    ).astype(jnp.float32)
    outputs = (input_f + branch).astype(jnp.bfloat16)
    row_start = seq_index * residual_rows + ch_index * local_rows
    window_index = window_lookup(row_start, every_bin_list)
    window_ids = jnp.arange(species.shape[0], dtype=jnp.int32)
    my_species = jnp.sum(jnp.where(window_ids == window_index, species, 0))
    is_human = my_species == 0
    targets = counts.astype(jnp.float32)
    zero_human = jnp.zeros((local_rows, HUMAN), jnp.bfloat16)
    zero_mouse = jnp.zeros((local_rows, MOUSE), jnp.bfloat16)
    start_logits = (
        jnp.zeros((local_rows, HUMAN), jnp.float32),
        jnp.zeros((local_rows, MOUSE), jnp.float32),
    )
    piece = lax.all_gather(head_weight, "ch", axis=0, tiled=True)

    def human_add(unused):
        return (
            jnp.dot(outputs, piece[:, :HUMAN], preferred_element_type=jnp.float32),
            start_logits[1],
        )

    def mouse_add(unused):
        return (
            start_logits[0],
            jnp.dot(outputs, piece[:, HUMAN:], preferred_element_type=jnp.float32),
        )

    logit_sums = lax.cond(is_human, human_add, mouse_add, 0)

    def human_grads(unused):
        return (poisson_grad(logit_sums[0] + head_bias[:HUMAN], targets), zero_mouse)

    def mouse_grads(unused):
        return (zero_human, poisson_grad(logit_sums[1] + head_bias[HUMAN:], targets[:, :MOUSE]))

    grad_human, grad_mouse = lax.cond(is_human, human_grads, mouse_grads, 0)

    def back_piece(piece):

        def human_back(unused):
            return lax.dot_general(
                grad_human, piece[:, :HUMAN], contract_cols, preferred_element_type=jnp.float32
            )

        def mouse_back(unused):
            return lax.dot_general(
                grad_mouse, piece[:, HUMAN:], contract_cols, preferred_element_type=jnp.float32
            )

        return lax.cond(is_human, human_back, mouse_back, 0)

    grad_out = back_piece(lax.all_gather(head_weight, "ch", axis=0, tiled=True))

    def human_term(unused):
        part = lax.dot_general(
            outputs, grad_human, contract_rows, preferred_element_type=jnp.float32
        )
        return jnp.concatenate(
            [
                part,
                jnp.zeros(
                    (lax.axis_size(("seq", "ch")) * (width // (seq_count * ch_count)), MOUSE),
                    jnp.float32,
                ),
            ],
            1,
        )

    def mouse_term(unused):
        part = lax.dot_general(
            outputs, grad_mouse, contract_rows, preferred_element_type=jnp.float32
        )
        return jnp.concatenate(
            [
                jnp.zeros(
                    (lax.axis_size(("seq", "ch")) * (width // (seq_count * ch_count)), HUMAN),
                    jnp.float32,
                ),
                part,
            ],
            1,
        )

    head_weight_grad = lax.psum_scatter(
        lax.cond(is_human, human_term, mouse_term, 0),
        ("seq", "ch"),
        scatter_dimension=0,
        tiled=True,
    )
    bias_part = jnp.concatenate(
        [jnp.sum(grad_human.astype(jnp.float32), 0), jnp.sum(grad_mouse.astype(jnp.float32), 0)]
    )
    grad_branch = grad_out.astype(jnp.bfloat16)
    mix_piece = lax.all_gather(grad_branch, "ch", axis=0, tiled=True)
    grad_rows = lax.dot_general(
        mix_piece, mix_weight, contract_cols, preferred_element_type=jnp.float32
    )
    grad_acts = grad_rows
    mix_part = lax.dot_general(
        act_two, mix_piece, contract_rows, preferred_element_type=jnp.float32
    )
    grad_pre_two = gelu_grad(pre_two, grad_acts)
    gain_part = jnp.sum(grad_pre_two * normed_two, 0)
    shift_part = jnp.sum(grad_pre_two, 0)
    gain_two_grad, shift_two_grad = lax.psum((gain_part, shift_part), "seq")
    convolution_gradient = (
        gain_two
        * scale_two
        * (grad_pre_two - shift_two_grad * inv_bins - normed_two * gain_two_grad * inv_bins)
    ).astype(jnp.bfloat16)
    padded_gradient = with_halo(convolution_gradient, (("seq", 0),), DILATION_STEP)
    conv_part = jnp.stack(
        [
            lax.dot_general(
                padded_input[
                    kernel_tap_index * DILATION_STEP : kernel_tap_index * DILATION_STEP
                    + residual_rows
                ],
                jnp.where(
                    fwd_masks[kernel_tap_index][:, None],
                    convolution_gradient,
                    jnp.zeros_like(convolution_gradient),
                ),
                contract_rows,
                preferred_element_type=jnp.float32,
            )
            for kernel_tap_index in range(TAPS)
        ]
    )
    total = jnp.zeros((lax.axis_size("ch") * local_rows, width), jnp.float32)
    for kernel_tap_index in range(TAPS):
        grad_rows = lax.dynamic_slice_in_dim(
            padded_gradient,
            (2 - kernel_tap_index) * DILATION_STEP,
            lax.axis_size("ch") * local_rows,
            0,
        )
        product = lax.dot_general(
            grad_rows,
            conv_weight[kernel_tap_index],
            contract_cols,
            preferred_element_type=jnp.float32,
        )
        total = total + product * back_masks[kernel_tap_index]
    grad_act_one = lax.psum_scatter(
        total.astype(jnp.bfloat16), "ch", scatter_dimension=0, tiled=True
    ).astype(jnp.float32)
    grad_pre_one = gelu_grad(pre_one, grad_act_one)
    gain_one_grad, shift_one_grad, head_bias_grad = lax.psum(
        (jnp.sum(grad_pre_one * normed_one, 0), jnp.sum(grad_pre_one, 0), bias_part), ("seq", "ch")
    )
    input_grad = grad_out + gain_one * scale_one * (
        grad_pre_one - shift_one_grad * inv_bins - normed_one * gain_one_grad * inv_bins
    )
    conv_weight_grad, mix_weight_grad = lax.psum((conv_part, mix_part), "seq")
    return (
        outputs,
        input_grad,
        gain_one_grad,
        shift_one_grad,
        conv_weight_grad,
        gain_two_grad,
        shift_two_grad,
        mix_weight_grad,
        head_weight_grad,
        head_bias_grad,
    )


def solution(mesh):
    in_specs = (
        P(("seq", "ch"), None),
        P(),
        P(),
        P(None, None, "ch"),
        P("ch"),
        P("ch"),
        P("ch", None),
        P("ch", None),
        P(),
        P(),
        P(("seq", "ch"), None),
    )
    out_specs = (
        P(("seq", "ch"), None),
        P(("seq", "ch"), None),
        P(),
        P(),
        P(None, None, "ch"),
        P("ch"),
        P("ch"),
        P("ch", None),
        P(("seq", "ch"), None),
        P(),
    )
    return jax.shard_map(
        on_device, mesh=mesh, in_specs=in_specs, out_specs=out_specs, check_vma=False
    )
```

profile of v0, /device:TPU:0, one launch (start us, length us, event | category | flops | bytes accessed | tf_op | source)
XLA Modules:
  0.0 631.1 jit_solution(14036912105792922197)
XLA Ops:
  8.4 42.1 %all-reduce.4 = (f32[768]{0:T(1024)S(1)}, f32[768]{0:T(1024)S(1)}) all-reduce(f32[768]{0:T(1024)S(1)} %get-tuple-element.95, f32[768]{0:T(1024)S(1)} %get-tuple-element.94), channel_id=1, replica_groups=mesh['seq'=8,'ch'=4] {'seq','ch'}, use_global_device_ids=true, to_apply=%region_3.0 | all-reduce | flops 1536 | bytes 12288 | tf_op jit(solution)/shard_map/psum | solution.py:73
  51.2 2.1 fusion.33
  53.5 19.5 %all-gather.4.cloned.1.call-done = bf16[1024,768]{1,0:T(8,128)(2,1)} async-done(((bf16[256,768]{1,0:T(8,128)(2,1)}), bf16[1024,768]{1,0:T(8,128)(2,1)}) %all-gather.4.cloned.1.call-update) | async-done | bytes 1572880 | tf_op jit(solution)/shard_map/all_gather | solution.py:81
  75.3 3.2 collective-permute-start.1
  80.6 2.0 convolution_select_fusion
  83.4 21.6 %all-reduce.6 = (f32[96]{0:T(128)S(1)}, f32[96]{0:T(128)S(1)}) all-reduce(f32[96]{0:T(128)S(1)} %get-tuple-element.93, f32[96]{0:T(128)S(1)} %get-tuple-element.92), channel_id=1, replica_groups=mesh['seq'=8,'ch'=4] {'seq'}, use_global_device_ids=true, to_apply=%region_7.8 | all-reduce | flops 192 | bytes 1536 | tf_op jit(solution)/shard_map/psum | solution.py:107
  109.2 6.3 copy.26
  115.4 5.3 convert_element_type.74
  120.8 10.6 %reduce-scatter.6.cloned.1.call-done = bf16[256,768]{1,0:T(8,128)(2,1)} async-done(((bf16[1024,768]{1,0:T(8,128)(2,1)}), bf16[256,768]{1,0:T(8,128)(2,1)}) %reduce-scatter.6.cloned.1.call-update) | async-done | bytes 393232 | tf_op jit(solution)/shard_map/reduce_scatter | solution.py:113
  133.2 71.8 %all-gather.6.cloned.1.call-done = bf16[768,6956]{1,0:T(8,128)(2,1)} async-done(((bf16[192,6956]{1,0:T(8,128)(2,1)}), bf16[768,6956]{1,0:T(8,128)(2,1)}) %all-gather.6.cloned.1.call-update) | async-done | bytes 10684432 | tf_op jit(solution)/shard_map/all_gather | solution.py:170
  204.9 5.9 conditional.4
  204.9 5.8 fusion.2
  210.9 7.6 %conditional.5 = (bf16[256,5313]{1,0:T(8,128)(2,1)S(1)}, bf16[256,1643]{1,0:T(8,128)(2,1)}) conditional(s32[]{:T(128)} %convert_element_type.73, (f32[6956]{0:T(1024)S(1)}, f32[256,1643]{0,1:T(8,128)S(1)}, f32[256,5313]{1,0:T(8,128)}) %tuple.87, (f32[6956]{0:T(1024)S(1)}, f32[256,5313]{1,0:T(8,128)S(1)}, f32[256,5313]{1,0:T(8,128)}) %tuple.88), branch_computations={%region_12.13_spmd, %region_13.14_spmd} | conditional | flops 19041792 | bytes 17040690 | solution.py:154
  211.1 6.4 %fusion.11 = bf16[256,5313]{1,0:T(8,128)(2,1)S(1)} fusion(f32[256,5313]{1,0:T(8,128)} %get-tuple-element.51, f32[256,5313]{1,0:T(8,128)S(1)} %get-tuple-element.49, f32[5313]{0:T(1024)S(1)} %slice.45), kind=kLoop, calls=%fused_computation.13 | loop fusion | flops 19041792 | bytes 13622532 | tf_op jit(solution)/shard_map/cond/branch_1_fun/convert_element_type | solution.py:46
  218.5 6.6 %conditional.6 = (f32[256,768]{1,0:T(8,128)}) conditional(s32[]{:T(128)} %convert_element_type.73, (bf16[768,6956]{1,0:T(8,128)(2,1)}, bf16[256,1643]{1,0:T(8,128)(2,1)}) %tuple.39, (bf16[768,6956]{1,0:T(8,128)(2,1)}, bf16[256,5313]{1,0:T(8,128)(2,1)S(1)}) %tuple.40), branch_computations={%region_14.15_spmd, %region_15.16_spmd} | conditional | flops 2089156608 | bytes 11764232 | solution.py:168
  218.5 6.6 %fusion.14 = f32[256,768]{1,0:T(8,128)} fusion(bf16[256,5313]{1,0:T(8,128)(2,1)S(1)} %get-tuple-element.54, bf16[768,6956]{1,0:T(8,128)(2,1)} %get-tuple-element.55), kind=kOutput, calls=%fused_computation.16 | convolution fusion | flops 2089156608 | bytes 11764224 | tf_op jit(solution)/shard_map/cond/branch_1_fun/dot_general | solution.py:159
  227.1 19.7 %all-gather.8.cloned.1.call-done = bf16[1024,768]{1,0:T(8,128)(2,1)} async-done(((bf16[256,768]{1,0:T(8,128)(2,1)}), bf16[1024,768]{1,0:T(8,128)(2,1)}) %all-gather.8.cloned.1.call-update) | async-done | bytes 1572880 | tf_op jit(solution)/shard_map/all_gather | solution.py:212
  246.8 3.0 fusion.96
  249.8 21.4 %all-reduce.5 = (f32[96]{0:T(128)S(1)}, f32[96]{0:T(128)S(1)}) all-reduce(f32[96]{0:T(128)S(1)} %get-tuple-element.91, f32[96]{0:T(128)S(1)} %get-tuple-element.90), channel_id=1, replica_groups=mesh['seq'=8,'ch'=4] {'seq'}, use_global_device_ids=true, to_apply=%region_19.20 | all-reduce | flops 192 | bytes 1536 | tf_op jit(solution)/shard_map/psum | solution.py:223
  274.2 2.1 collective-permute-start.3
  277.3 3.5 collective-permute-done.3
  280.8 2.2 add_convert_fusion
  283.2 2.1 convolution_bitcast_fusion.2
  288.7 13.4 %conditional.7 = (f32[768,6956]{0,1:T(8,128)}) conditional(s32[]{:T(128)} %convert_element_type.73, (bf16[256,768]{1,0:T(8,128)(2,1)}, bf16[256,1643]{1,0:T(8,128)(2,1)}) %tuple.41, (bf16[256,768]{1,0:T(8,128)(2,1)}, bf16[256,5313]{1,0:T(8,128)(2,1)S(1)}) %tuple.42), branch_computations={%region_27.28_spmd, %region_28.29_spmd} | conditional | flops 2089156608 | bytes 57125388 | solution.py:203
  288.7 3.3 fusion.103
  292.0 10.1 %concatenate.17 = f32[768,6956]{0,1:T(8,128)} pad(f32[768,5313]{0,1:T(8,128)S(1)} %fusion.103, f32[]{:T(128)} %constant.157.clone), padding=0_0x0_1643 | pad | bytes 37690372 | tf_op jit(solution)/shard_map/cond/branch_1_fun/concatenate | solution.py:176
  302.1 21.4 %copy.28 = f32[768,6956]{1,0:T(8,128)} copy(f32[768,6956]{0,1:T(8,128)} %get-tuple-element.145) | data formatting | bytes 42737664 | tf_op jit(solution)/shard_map/cond | solution.py:203
  327.2 38.1 %all-reduce.3 = (f32[768]{0:T(1024)S(1)}, f32[768]{0:T(1024)S(1)}, f32[6956]{0:T(1024)}) all-reduce(f32[768]{0:T(1024)S(1)} %get-tuple-element.89, f32[768]{0:T(1024)S(1)} %get-tuple-element.88, f32[6956]{0:T(1024)S(1)} %pad_maximum_fusion.11), channel_id=1, replica_groups=mesh['seq'=8,'ch'=4] {'seq','ch'}, use_global_device_ids=true, to_apply=%region_24.25 | all-reduce | flops 8492 | bytes 67936 | tf_op jit(solution)/shard_map/psum | solution.py:267
  365.2 2.3 fusion.38
  367.5 24.2 %all-reduce.10.cloned.1.call-done = (f32[3,768,96]{1,2,0:T(8,128)}, f32[96,768]{1,0:T(8,128)}) async-done(((f32[3,768,96]{1,2,0:T(8,128)}, f32[96,768]{1,0:T(8,128)}), (f32[3,768,96]{1,2,0:T(8,128)}, f32[96,768]{1,0:T(8,128)})) %all-reduce.10.cloned.1.call-update) | async-done | bytes 1179664 | tf_op jit(solution)/shard_map/psum | solution.py:273
  391.7 228.6 %reduce-scatter.10.cloned.1.call-done = f32[24,6956]{1,0:T(8,128)} async-done(((f32[768,6956]{1,0:T(8,128)}), f32[24,6956]{1,0:T(8,128)}) %reduce-scatter.10.cloned.1.call-update) | async-done | bytes 667792
  620.4 2.1 copy.44
  (98 shorter events, 28.3 us)
Async XLA Ops:
  7.2 97.9 %copy-start = (bf16[96,768]{1,0:T(8,128)(2,1)S(1)}, bf16[96,768]{1,0:T(8,128)(2,1)}, u32[]{:S(2)}) copy-start(bf16[96,768]{1,0:T(8,128)(2,1)} %param.25) | copy-start | bytes 442372
  7.2 73.4 %copy-start.8 = (bf16[3,768,96]{1,2,0:T(8,128)(2,1)S(1)}, bf16[3,768,96]{1,2,0:T(8,128)(2,1)}, u32[]{:S(2)}) copy-start(bf16[3,768,96]{1,2,0:T(8,128)(2,1)} %param.22) | copy-start | bytes 1327108
  7.2 65.8 %all-gather.4.cloned.1.call-start = ((), (), s32[]{:S(2)}) async-start(), calls=%async_computation.3 | async-start | bytes 1966080 | tf_op jit(solution)/shard_map/all_gather | solution.py:81
  53.4 77.9 %reduce-scatter.6.cloned.1.call-start = ((), (), s32[]{:S(2)}) async-start(), calls=%async_computation.4 | async-start | bytes 1966080 | tf_op jit(solution)/shard_map/reduce_scatter | solution.py:113
  73.8 8.9 %collective-permute-start = (bf16[11,768]{1,0:T(8,128)(2,1)S(1)}, bf16[11,768]{1,0:T(8,128)(2,1)S(1)}, u32[]{:S(2)}, u32[]{:S(2)}) collective-permute-start(bf16[11,768]{1,0:T(8,128)(2,1)S(1)} %get-tuple-element.109), channel_id=1, source_target_pairs={{0,4},{4,8},{8,12},{12,16},{16,20},{20,24},{24,28},{28,0},{1,5},{5... | collective-permute-start | bytes 50696 | tf_op jit(solution)/shard_map/ppermute | solution.py:26
  75.3 7.4 %copy-start.4 = (bf16[1024,768]{1,0:T(8,128)(2,1)S(1)}, bf16[1024,768]{1,0:T(8,128)(2,1)}, u32[]{:S(2)}) copy-start(bf16[1024,768]{1,0:T(8,128)(2,1)} %all-gather.4.cloned.1.call-done) | copy-start | bytes 4718596
  75.3 5.3 collective-permute-start.1
  80.6 2.8 copy-start.21
  82.6 22.4 %copy-start.15 = (f32[96]{0:T(128)S(1)}, f32[96]{0:T(128)}, u32[]{:S(2)}) copy-start(f32[96]{0:T(128)} %param.23) | copy-start | bytes 1156
  82.6 22.4 %copy-start.17 = (f32[96]{0:T(128)S(1)}, f32[96]{0:T(128)}, u32[]{:S(2)}) copy-start(f32[96]{0:T(128)} %param.24) | copy-start | bytes 1156
  82.6 24.4 %copy-start.19 = (bf16[11,768]{1,0:T(8,128)(2,1)}, bf16[11,768]{1,0:T(8,128)(2,1)S(1)}, u32[]{:S(2)}) copy-start(bf16[11,768]{1,0:T(8,128)(2,1)S(1)} %collective-permute-done) | copy-start | bytes 50692
  83.4 24.4 %copy-start.6 = (f32[1024,96]{0,1:T(8,128)}, f32[1024,96]{0,1:T(8,128)S(1)}, u32[]{:S(2)}) copy-start(f32[1024,96]{0,1:T(8,128)S(1)} %get-tuple-element.119) | copy-start | bytes 1179652
  105.0 2.8 copy-start.23
  107.0 97.9 %all-gather.6.cloned.1.call-start = ((), (), s32[]{:S(2)}) async-start(), calls=%async_computation.5 | async-start | bytes 13516800 | tf_op jit(solution)/shard_map/all_gather | solution.py:170
  107.8 139.0 %all-gather.8.cloned.1.call-start = ((), (), s32[]{:S(2)}) async-start(), calls=%async_computation.6 | async-start | bytes 1966080 | tf_op jit(solution)/shard_map/all_gather | solution.py:212
  115.4 15.9 %copy-start.2 = (bf16[256,768]{1,0:T(8,128)(2,1)S(1)}, bf16[256,768]{1,0:T(8,128)(2,1)}, u32[]{:S(2)}) copy-start(bf16[256,768]{1,0:T(8,128)(2,1)} %param.19) | copy-start | bytes 1179652
  204.9 5.9 copy-start.10
  227.0 98.4 %reduce-scatter.8.cloned.1.call-start = ((), (), s32[]{:S(2)}) async-start(), calls=%async_computation.7 | async-start | bytes 1966080 | tf_op jit(solution)/shard_map/reduce_scatter | solution.py:263
  271.2 6.1 copy-start.16
  271.2 6.1 copy-start.24
  271.2 5.3 copy-start.9
  272.6 3.9 collective-permute-start.2
  274.2 6.6 %collective-permute-start.3 = (bf16[11,96]{0,1:T(8,128)(2,1)S(1)}, bf16[11,96]{0,1:T(8,128)(2,1)S(1)}, u32[]{:S(2)}, u32[]{:S(2)}) collective-permute-start(bf16[11,96]{0,1:T(8,128)(2,1)S(1)} %get-tuple-element.111), channel_id=1, source_target_pairs={{0,4},{4,8},{8,12},{12,16},{16,20},{20,24},{24,28},{28,0},{1,5},{5... | collective-permute-start | bytes 6344 | tf_op jit(solution)/shard_map/ppermute | solution.py:26
  280.7 2.5 copy-start.20
  282.9 2.4 copy-start.22
  282.9 108.8 %all-reduce.10.cloned.1.call-start = ((), (), s32[]{:S(2)}) async-start(), calls=%async_computation.9 | async-start | bytes 2359296 | tf_op jit(solution)/shard_map/psum | solution.py:273
  283.2 2.1 copy-start.5
  285.4 2.0 copy-start.7
  288.6 331.8 %reduce-scatter.10.cloned.1.call-start = ((), (), s32[]{:S(2)}) async-start(), calls=%async_computation.8 | async-start | bytes 22302720
  325.4 298.9 %copy-start.1 = (bf16[96,768]{1,0:T(8,128)(2,1)S(1)}, bf16[96,768]{1,0:T(8,128)(2,1)}, u32[]{:S(2)}) copy-start(bf16[96,768]{1,0:T(8,128)(2,1)} %param.25) | copy-start | bytes 442372
  365.2 259.0 %copy-start.13 = (f32[768]{0:T(1024)}, f32[768]{0:T(1024)S(1)}, u32[]{:S(2)}) copy-start(f32[768]{0:T(1024)S(1)} %get-tuple-element.134) | copy-start | bytes 9220
  365.2 259.0 %copy-start.14 = (f32[768]{0:T(1024)}, f32[768]{0:T(1024)S(1)}, u32[]{:S(2)}) copy-start(f32[768]{0:T(1024)S(1)} %get-tuple-element.135) | copy-start | bytes 9220
  (3 other events, 5.7 us)
Sparse Core Ops, SparseCore 0:
  53.5 19.4 all-gather.3
  107.1 24.1 reduce-scatter.5
  132.9 72.0 all-gather.5
  227.1 19.6 all-gather.7
  283.1 24.3 reduce-scatter.7
  311.4 80.2 all-reduce.9
  398.7 221.6 reduce-scatter.9
where the time goes:
time: 632 us; the launch traced here: 631 us
  waiting for transfers between devices  379 us (60%)
  blocking collectives  123 us (19%)
  local copies, waits for them, and re-layouts  43.6 us (7%)
  matrix products  34.1 us (5%)
  other arithmetic  28.4 us (4%)
  between operations  15.2 us (2%)
  starting transfers between devices  7.34 us (1%)
    unnamed x8, waiting for transfers between devices  229 us
    all_gather x1, waiting for transfers between devices, on_device(): grad_out = back_piece(lax.all_gather(head_weight, 'ch', axis=0, tiled=True))  71.8 us
    psum x1, blocking collectives, on_device(): lax.psum((jnp.sum(input_f, 0), jnp.sum(input_f * input_f, 0)), ('seq', 'c...  42.1 us
    psum x1, blocking collectives, on_device(): lax.psum((jnp.sum(grad_pre_one * normed_one, 0), jnp.sum(grad_pre_one, 0)...  38.1 us
    psum x1, waiting for transfers between devices, on_device(): conv_weight_grad, mix_weight_grad = lax.psum((conv_part, mix_part), 'seq')  24.2 us
    psum x1, blocking collectives, on_device(): lax.psum((jnp.sum(conv_out, 0), jnp.sum(conv_out * conv_out, 0)), 'seq')  21.6 us
    cond x1, local copies, waits for them, and re-layouts, on_device(): lax.cond(is_human, human_term, mouse_term, 0)  21.4 us
    psum x1, blocking collectives, on_device(): gain_two_grad, shift_two_grad = lax.psum((gain_part, shift_part), 'seq')  21.4 us
  transfers between devices with their start and end apart: 11, of which 8 were waited for; matrix products, arithmetic and copies ran while one was open for 11% of the time, Pallas kernels for 0%

commit v1 on v0

--- a/solution.py
+++ b/solution.py
@@ -1,6 +1,8 @@
 import jax
 import jax.numpy as jnp
 from jax import lax
+from jax.experimental import pallas as pl
+from jax.experimental.pallas import tpu as pltpu
 from jax.sharding import PartitionSpec as P
 
 HUMAN = 5313
@@ -285,6 +287,634 @@
     )
 
 
+F32 = jnp.float32
+BF16 = jnp.bfloat16
+TILE = 384
+MESH_ID = pl.DeviceIdType.MESH
+GELU_C = 0.7978845608028654
+GELU_A = 0.044715
+
+
+def gelu_of(v):
+    return 0.5 * v * (1.0 + jnp.tanh(GELU_C * (v + GELU_A * v * v * v)))
+
+
+def gelu_slope(v):
+    t = jnp.tanh(GELU_C * (v + GELU_A * v * v * v))
+    return 0.5 * (1.0 + t) + 0.5 * v * (1.0 - t * t) * (GELU_C * (1.0 + 3.0 * GELU_A * v * v))
+
+
+def logit_slope(z, n):
+    e = jnp.exp(-jnp.abs(z))
+    u = 1.0 + e
+    log_u = jnp.log(u)
+    small = e < 0.01
+    series = 1.0 - e * (0.5 - e * (1.0 / 3.0 - e * (0.25 - 0.2 * e)))
+    plus = z >= 0.0
+    tail = jnp.where(small, series, log_u)
+    rate = jnp.where(plus, z + jnp.where(small, e * series, log_u), tail)
+    top = jnp.where(plus, 1.0, e)
+    num = jnp.where(small, 1.0, top)
+    return (top * rate - n * num) / (u * rate)
+
+
+def tree(parts):
+    while len(parts) > 1:
+        parts = [parts[i] + parts[i + 1] for i in range(0, len(parts), 2)]
+    return parts[0]
+
+
+def dot_nn(a, b):
+    return jnp.dot(a, b, preferred_element_type=F32)
+
+
+def dot_nt(a, b):
+    return lax.dot_general(a, b, (((1,), (1,)), ((), ())), preferred_element_type=F32)
+
+
+def flip(i, unit):
+    return i + unit - 2 * unit * ((i // unit) % 2)
+
+
+def step_kernel(
+    x_ref, p1_ref, g2_ref, cwo_ref, w_ref, wm_ref, cs_ref, bv_ref, flag_ref,
+    out_ref, ig_ref, s1_ref, s2_ref, cg_ref, oh_ref, om_ref, bg_ref,
+    act, hin, cw, conv, tap0, tap2, wh, wm, wsel, cnt, orow, ocol, gs, gacc, grecv,
+    pbuf, r1, b1, r2, b2, r3, b3, r4, fin, frecv,
+    m1, m2, m3, m4, a1, a2, a3, a4, z1, z2, z3, z4, q1, q2, q3, q4,
+    bl, bxy, bs, bz, gpad, gsend, ghalo, gk, act2, cgb, crc, csc, crx, csx, cry, csy, crz, csz, crw, cao,
+    st_s, st_r, hs_s, hs_r, cw_s, cw_r, wl_s, ws_s, ws_r, wx_s, wx_r, wy_s, wy_r, ct_l, ct_s, ct_r,
+    ox_s, ox_r, rs_s, rs_r, fx_s, fx_r, bx_s, bx_r, gh_s, gh_r, cg_s, cg_r,
+):
+    seq = lax.axis_index("seq")
+    ch = lax.axis_index("ch")
+    nseq = lax.axis_size("seq")
+    rows = x_ref.shape[0]
+    k = ch % 2
+    xb = ch // 2
+    yb = seq % 2
+    z0 = (seq // 2) % 2
+    z1b = (seq // 4) % 2
+    inv = 1.0 / (rows * nseq * 4)
+    sib = (seq, ch + 1 - 2 * k)
+    xpeer = (seq, flip(ch, 2))
+    ypeer = (flip(seq, 1), ch)
+    zpeers = ((flip(seq, 2), ch), (flip(seq, 4), ch), (flip(flip(seq, 2), 4), ch))
+    near = []
+    for r in range(1, 8):
+        c = flip(ch, 1) if r % 2 else ch
+        c = flip(c, 2) if (r // 2) % 2 else c
+        near.append((flip(seq, 1) if r // 4 else seq, c))
+    line = seq * 4 + ch
+    after = (line + 1) % (nseq * 4)
+    before = (line + nseq * 4 - 1) % (nseq * 4)
+    after_id = (after // 4, after % 4)
+    before_id = (before // 4, before % 4)
+
+    def rcopy(src, dst, ss, rs, who):
+        return pltpu.make_async_remote_copy(
+            src_ref=src, dst_ref=dst, send_sem=ss, recv_sem=rs, device_id=who, device_id_type=MESH_ID
+        )
+
+    sent = []
+
+    def go(copy):
+        copy.start()
+        sent.append(copy)
+        return copy
+
+    barrier = pltpu.get_barrier_semaphore()
+    for who in [*near, *zpeers, after_id, before_id]:
+        pl.semaphore_signal(barrier, inc=1, device_id=who, device_id_type=MESH_ID)
+
+    def small_start(i, msg, slots):
+        return [go(rcopy(msg, slots.at[r], st_s.at[i, r], st_r.at[i, r], near[r])) for r in range(7)]
+
+    def small_mid(i, copies, msg, slots, mid, zslots):
+        for c in copies:
+            c.wait_recv()
+        mid[...] = tree([msg[...]] + [slots[r] for r in range(7)])
+        return [go(rcopy(mid, zslots.at[r], st_s.at[i, 7 + r], st_r.at[i, 7 + r], zpeers[r])) for r in range(3)]
+
+    def small_end(copies, mid, zslots):
+        for c in copies:
+            c.wait_recv()
+        return tree([mid[...]] + [zslots[r] for r in range(3)])
+
+    own_rows = pl.ds(pl.multiple_of(192 * ch, 192), 192)
+
+    def human_cols(j, half):
+        return pl.ds(pl.multiple_of(2688 * half + TILE * j, 128), TILE)
+
+    def mouse_cols(j, half):
+        return pl.ds(pl.multiple_of(896 * half + TILE * j, 128), TILE if j < 2 else 128)
+
+    def w_src(t, half):
+        return w_ref.at[:, human_cols(t, half)] if t < 7 else wm_ref.at[:, mouse_cols(t - 7, half)]
+
+    def w_dst(t, block):
+        rows_at = pl.ds(pl.multiple_of(192 * block, 192), 192)
+        if t < 7:
+            return wh.at[t, rows_at, :]
+        return wm.at[t - 7, rows_at, :] if t < 9 else wm.at[2, rows_at, pl.ds(0, 128)]
+
+    order = (0, 7, 1, 8, 2, 9, 3, 4, 5, 6)
+    wm[2, :, 128:] = jnp.zeros((768, TILE - 128), BF16)
+    local = []
+    for t in order:
+        c = pltpu.make_async_copy(w_src(t, k), w_dst(t, ch), wl_s.at[t])
+        c.start()
+        local.append(c)
+    my_bins = pl.ds(pl.multiple_of(rows * k, rows), rows)
+    for j in range(7):
+        c = pltpu.make_async_copy(cs_ref.at[k, :, pl.ds(TILE * j, TILE)], cnt.at[j, my_bins, :], ct_l.at[j])
+        c.start()
+        local.append(c)
+    own_cw = pl.ds(pl.multiple_of(96 * ch, 96), 96)
+    c = pltpu.make_async_copy(cwo_ref, cw.at[own_cw, :], cw_s.at[5])
+    c.start()
+    local.append(c)
+    xf = x_ref[...].astype(F32)
+    xs = jnp.sum(xf, 0, keepdims=True)
+    xq = jnp.sum(xf * xf, 0, keepdims=True)
+    m1[0:1, :] = xs[:, :TILE]
+    m1[1:2, :] = xs[:, TILE:]
+    m1[2:3, :] = xq[:, :TILE]
+    m1[3:4, :] = xq[:, TILE:]
+    m1[4:6, :] = g2_ref[...]
+    m1[6:8, :] = jnp.zeros((2, TILE), F32)
+    pl.semaphore_wait(barrier, 12)
+
+    e1 = small_start(0, m1, a1)
+    cw_sib = go(rcopy(cwo_ref, cw.at[own_cw, :], cw_s.at[0], cw_r.at[0], sib))
+
+    def half_rows(c, h):
+        return pl.ds(pl.multiple_of(96 * c + 48 * h, 48), 48)
+
+    cw_x = go(rcopy(cwo_ref.at[pl.ds(pl.multiple_of(48 * yb, 48), 48), :], cw.at[half_rows(ch, yb), :], cw_s.at[1], cw_r.at[1], xpeer))
+    xch = flip(ch, 2)
+    wx = {}
+
+    def send_w(t):
+        who = (seq, flip(ch, 2) + yb * (1 - 2 * k))
+        half = k + yb * (1 - 2 * k)
+        wx[t] = go(rcopy(w_src(t, half), w_dst(t, ch), wx_s.at[t], wx_r.at[t], who))
+
+    wsib = {}
+
+    def send_w_sib(t):
+        wsib[t] = go(rcopy(w_src(t, 1 - k), w_dst(t, ch), ws_s.at[t], ws_r.at[t], sib))
+
+    wy = {}
+
+    def pass_w(t):
+        wx[t].wait_recv()
+        block = xch + yb * (1 - 2 * k)
+        wy[t] = go(rcopy(w_dst(t, block), w_dst(t, block), wy_s.at[t], wy_r.at[t], ypeer))
+
+    for t in order[:2]:
+        send_w_sib(t)
+    e1 = small_mid(0, e1, m1, a1, q1, z1)
+    send_w(order[0])
+    cw_x.wait_recv()
+    cw_y = go(rcopy(cw.at[half_rows(xch, yb), :], cw.at[half_rows(xch, yb), :], cw_s.at[2], cw_r.at[2], ypeer))
+    cw_f = go(rcopy(cw.at[half_rows(xch, yb), :], cw.at[half_rows(xch, yb), :], cw_s.at[3], cw_r.at[3], sib))
+    tot = small_end(e1, q1, z1)
+    mean1 = jnp.concatenate([tot[0:1], tot[1:2]], 1) * inv
+    scale1 = lax.rsqrt(jnp.concatenate([tot[2:3], tot[3:4]], 1) * inv - mean1 * mean1 + norm_eps)
+    gain2 = tot[4:5] * (1.0 / nseq)
+    shift2 = tot[5:6] * (1.0 / nseq)
+    gain1 = p1_ref[0:1, :]
+    shift1 = p1_ref[1:2, :]
+
+    def act_rows(i, _):
+        at = pl.ds(pl.multiple_of(i * 32, 32), 32)
+        v = (x_ref[at, :].astype(F32) - mean1) * scale1 * gain1 + shift1
+        act[at, :] = gelu_of(v).astype(BF16)
+        return 0
+
+    lax.fori_loop(0, rows // 32, act_rows, 0)
+    h_up = go(rcopy(act.at[pl.ds(0, 16), :], hin.at[1], hs_s.at[0], hs_r.at[0], before_id))
+    h_dn = go(rcopy(act.at[pl.ds(rows - 16, 16), :], hin.at[0], hs_s.at[1], hs_r.at[1], after_id))
+    send_w(order[1])
+    pass_w(order[0])
+    cw_y.wait_recv()
+    cw_g = go(rcopy(cw.at[half_rows(xch, 1 - yb), :], cw.at[half_rows(xch, 1 - yb), :], cw_s.at[4], cw_r.at[4], sib))
+    cw_sib.wait_recv()
+    cw_f.wait_recv()
+    cw_g.wait_recv()
+    local[17].wait()
+    start = line * rows - SHIFT + rows * nseq * 4
+    first = (start % WINDOW_BINS) == 0
+    last = ((start + rows) % WINDOW_BINS) == 0
+    keep0 = jnp.where(first, 0.0, 1.0)
+    keep2 = jnp.where(last, 0.0, 1.0)
+    mine = pl.ds(16, rows)
+    conv[...] = dot_nt(act[...], cw[:, 768:1536])
+    tap0[mine, :] = dot_nt(act[...], cw[:, 0:768])
+    tap2[mine, :] = dot_nt(act[...], cw[:, 1536:2304])
+    h_up.wait_recv()
+    h_dn.wait_recv()
+    tap0[0:16, :] = dot_nt(hin[0], cw[:, 0:768]) * keep0
+    tap2[pl.ds(rows + 16, 16), :] = dot_nt(hin[1], cw[:, 1536:2304]) * keep2
+    step = DILATION_STEP
+    full = conv[...] + tap0[pl.ds(16 - step, rows), :] + tap2[pl.ds(16 + step, rows), :]
+    conv[...] = full
+    m2[0:1, :] = jnp.sum(full, 0, keepdims=True)
+    m2[1:2, :] = jnp.sum(full * full, 0, keepdims=True)
+    e2 = small_start(1, m2, a2)
+    for t in order[2:4]:
+        send_w(t)
+        send_w_sib(t)
+    c_sib = []
+    for j in range(7):
+        c_sib.append(go(rcopy(cs_ref.at[1 - k, :, pl.ds(TILE * j, TILE)], cnt.at[j, my_bins, :], ct_s.at[j], ct_r.at[j], sib)))
+    e2 = small_mid(1, e2, m2, a2, q2, z2)
+    pass_w(order[1])
+    send_w(order[4])
+    tot2 = small_end(e2, q2, z2)
+    mean2 = tot2[0:1] * inv
+    scale2 = lax.rsqrt(tot2[1:2] * inv - mean2 * mean2 + norm_eps)
+
+    def mix_rows(i, _):
+        at = pl.ds(pl.multiple_of(i * 64, 64), 64)
+        v = (conv[at, :] - mean2) * scale2 * gain2 + shift2
+        a = gelu_of(v).astype(BF16)
+        act2[at, :] = a
+        o = (x_ref[at, :].astype(F32) + dot_nn(a, cw[:, 2304:])).astype(BF16)
+        out_ref[at, :] = o
+        orow[pl.ds(pl.multiple_of(rows * k + i * 64, 64), 64), :] = o
+        return 0
+
+    lax.fori_loop(0, rows // 64, mix_rows, 0)
+    o_x = go(rcopy(out_ref, orow.at[my_bins, :], ox_s.at[0], ox_r.at[0], sib))
+    for t in order[5:]:
+        send_w(t)
+    for t in order[4:]:
+        send_w_sib(t)
+    for t in order[2:4]:
+        pass_w(t)
+    o_x.wait_recv()
+    both = 2 * rows
+    ocol[...] = orow[...].T
+    gacc[...] = jnp.zeros((both, 768), F32)
+    bl[...] = jnp.zeros((16, TILE), F32)
+    human = flag_ref[0]
+    mouse = 1.0 - human
+
+    def head_tile(j, w_at):
+        bv = bv_ref[j]
+        total = jnp.zeros((1, TILE), F32)
+        for b in range(both // 128):
+            at = pl.ds(128 * b, 128)
+            z = dot_nn(orow[at, :], w_at[...]) + bv[0:1, :]
+            g = (logit_slope(z, cnt[j, at, :].astype(F32)) * bv[1:2, :]).astype(BF16)
+            gs[at, :] = g
+            total = total + jnp.sum(g.astype(F32), 0, keepdims=True)
+            gacc[at, :] = gacc[at, :] + dot_nt(g, w_at[...])
+        for b in range(4):
+            d = dot_nn(ocol[pl.ds(192 * b, 192), :], gs[...]).astype(BF16)
+            for y in range(2):
+                for xx in range(2):
+                    f = xx + k * (y - xx)
+                    g2 = y + k * (xx - y)
+                    pbuf[j, f, g2, b % 2, b // 2] = d[96 * y + 48 * xx:96 * y + 48 * xx + 48, :]
+        return total
+
+    f_me = xb + k * (yb - xb)
+    g_me = yb + k * (xb - yb)
+    peer_a = (seq + k * (1 - 2 * yb), ch + (1 - k) * (2 - 4 * xb))
+    peer_b = (seq + (1 - k) * (1 - 2 * yb), ch + k * (2 - 4 * xb))
+    rs1 = {}
+
+
+    for j in range(7):
+        t_need = (j, 7 + j) if j < 3 else (j,)
+        for t in order:
+            if t not in wy and order.index(t) <= order.index(t_need[-1]) + 2:
+                pass_w(t)
+        for t in t_need:
+            local[order.index(t)].wait()
+            wsib[t].wait_recv()
+            wy[t].wait_recv()
+        local[10 + j].wait()
+        c_sib[j].wait_recv()
+        if j < 3:
+            wsel[...] = (wh[j].astype(F32) * human + wm[j].astype(F32) * mouse).astype(BF16)
+            total = head_tile(j, wsel)
+            bl[8 + j:9 + j, :] = total * mouse
+        else:
+            total = head_tile(j, wh.at[j])
+        bl[j:j + 1, :] = total * human
+        rs1[j] = go(rcopy(pbuf.at[j, 1 - f_me], r1.at[j], rs_s.at[0, j], rs_r.at[0, j], peer_a))
+
+    hp = flag_ref[1]
+    mp = 1.0 - hp
+    rs2, rs3, rs4, rs5 = {}, {}, {}, {}
+
+    def adv1(j):
+        rs1[j].wait_recv()
+        own = pbuf[j, f_me].astype(F32)
+        got = r1[j].astype(F32)
+        b1[j] = (own * human + got * hp).astype(BF16)
+        ts = [j]
+        if j < 3:
+            b1[7 + j] = (own * mouse + got * mp).astype(BF16)
+            ts.append(7 + j)
+        for t in ts:
+            rs2[t] = go(rcopy(b1.at[t, 1 - g_me], r2.at[t], rs_s.at[1, t], rs_r.at[1, t], peer_b))
+
+    def adv2(t):
+        rs2[t].wait_recv()
+        b2[t] = (b1[t, g_me].astype(F32) + r2[t].astype(F32)).astype(BF16)
+        rs3[t] = go(rcopy(b2.at[t, 1 - z0], r3.at[t], rs_s.at[2, t], rs_r.at[2, t], zpeers[0]))
+
+    def adv3(t):
+        rs3[t].wait_recv()
+        b3[t] = (b2[t, z0].astype(F32) + r3[t].astype(F32)).astype(BF16)
+        rs4[t] = go(rcopy(b3.at[t, 1 - z1b], r4.at[t], rs_s.at[3, t], rs_r.at[3, t], zpeers[1]))
+
+    def adv4(t):
+        rs4[t].wait_recv()
+        fin[t] = b3[t, z1b].astype(F32) + r4[t].astype(F32)
+        rs5[t] = go(rcopy(fin.at[t, pl.ds(pl.multiple_of(24 - 24 * k, 8), 24), :], frecv.at[t], fx_s.at[t], fx_r.at[t], sib))
+
+    g_x = go(rcopy(gacc.at[pl.ds(pl.multiple_of(rows * (1 - k), rows), rows), :], grecv, gh_s.at[0], gh_r.at[0], sib))
+    bias_near = (near[1], near[3], near[5])
+    bx = [go(rcopy(bl, bxy.at[i], bx_s.at[i], bx_r.at[i], bias_near[i])) for i in range(3)]
+    g_x.wait_recv()
+
+    def back_rows(i, carry):
+        ga, sa = carry
+        at = pl.ds(pl.multiple_of(i * 64, 64), 64)
+        grad = gacc[pl.ds(pl.multiple_of(rows * k + i * 64, 64), 64), :] + grecv[at, :]
+        grecv[at, :] = grad
+        gb = grad.astype(BF16)
+        gs2 = dot_nt(gb, cw[:, 2304:])
+        nrm = (conv[at, :] - mean2) * scale2
+        gp = gs2 * gelu_slope(nrm * gain2 + shift2)
+        gpad[pl.ds(pl.multiple_of(16 + i * 64, 16), 64), :] = gp
+        return ga + jnp.sum(gp * nrm, 0, keepdims=True), sa + jnp.sum(gp, 0, keepdims=True)
+
+    zero_h = jnp.zeros((1, TILE), F32)
+    ga2, sa2 = lax.fori_loop(0, rows // 64, back_rows, (zero_h, zero_h))
+    m3[0:1, :] = ga2
+    m3[1:2, :] = sa2
+    e3 = small_start(2, m3, a3)
+
+    def keep_piece(value, first_piece):
+        low = value.astype(BF16)
+        for c in range(4):
+            for h in range(2):
+                p = first_piece + h
+                cgb[c % 2, c // 2, p // 4, (p // 2) % 2, p % 2] = low[96 * c:96 * c + 96, TILE * h:TILE * h + TILE]
+
+    for j in range(2):
+        adv1(j)
+    e3 = small_mid(2, e3, m3, a3, q3, z3)
+    keep_piece(dot_nn(act2[...].T, grecv[...].astype(BF16)), 6)
+    adv1(2)
+    adv1(3)
+    tot3 = small_end(e3, q3, z3)
+    s2_ref[...] = tot3
+    gg2 = tot3[0:1]
+    sg2 = tot3[1:2]
+
+    def conv_rows(i, _):
+        at = pl.ds(pl.multiple_of(i * 64, 64), 64)
+        into = pl.ds(pl.multiple_of(16 + i * 64, 16), 64)
+        nrm = (conv[at, :] - mean2) * scale2
+        gc = (gain2 * scale2 * (gpad[into, :] - sg2 * inv - nrm * gg2 * inv)).astype(BF16)
+        gsend[at, :] = gc
+        gpad[into, :] = gc.astype(F32)
+        return 0
+
+    lax.fori_loop(0, rows // 64, conv_rows, 0)
+    gh_up = go(rcopy(gsend.at[pl.ds(0, 16), :], ghalo.at[1], gh_s.at[1], gh_r.at[1], before_id))
+    gh_dn = go(rcopy(gsend.at[pl.ds(rows - 16, 16), :], ghalo.at[0], gh_s.at[2], gh_r.at[2], after_id))
+    adv1(4)
+    adv1(5)
+    adv2(0)
+    acc1 = dot_nn(gsend[...], cw[:, 768:1536])
+    keep_piece(dot_nn(gsend[...].T, act[...]), 2)
+    gh_up.wait_recv()
+    gh_dn.wait_recv()
+    gpad[0:16, :] = ghalo[0].astype(F32) * keep0
+    gpad[pl.ds(rows + 16, 16), :] = ghalo[1].astype(F32) * keep2
+    gk[0] = gpad[pl.ds(16 + step, rows), :].astype(BF16)
+    gk[1] = gpad[pl.ds(16 - step, rows), :].astype(BF16)
+    g_x.wait_send()
+    gacc[0:rows, :] = acc1 + dot_nn(gk[0], cw[:, 0:768]) + dot_nn(gk[1], cw[:, 1536:2304])
+
+    def first_rows(i, carry):
+        ga, sa = carry
+        at = pl.ds(pl.multiple_of(i * 32, 32), 32)
+        nrm = (x_ref[at, :].astype(F32) - mean1) * scale1
+        gp = gacc[at, :] * gelu_slope(nrm * gain1 + shift1)
+        gacc[at, :] = gp
+        return ga + jnp.sum(gp * nrm, 0, keepdims=True), sa + jnp.sum(gp, 0, keepdims=True)
+
+    zero_d = jnp.zeros((1, 768), F32)
+    ga1, sa1 = lax.fori_loop(0, rows // 32, first_rows, (zero_d, zero_d))
+    m4[0:1, :] = ga1[:, :TILE]
+    m4[1:2, :] = ga1[:, TILE:]
+    m4[2:3, :] = sa1[:, :TILE]
+    m4[3:4, :] = sa1[:, TILE:]
+    e4 = small_start(3, m4, a4)
+    keep_piece(dot_nn(gk[0].T, act[...]), 0)
+    keep_piece(dot_nn(gk[1].T, act[...]), 4)
+    c1 = go(rcopy(cgb.at[1 - k], crc, cg_s.at[0], cg_r.at[0], sib))
+    e4 = small_mid(3, e4, m4, a4, q4, z4)
+    adv1(6)
+
+    def add_into(dst, one, two):
+        dst[...] = (one.astype(F32) + two.astype(F32)).astype(BF16)
+
+    c1.wait_recv()
+    add_into(csc, cgb[k], crc[...])
+    c2 = go(rcopy(csc.at[1 - xb], crx, cg_s.at[1], cg_r.at[1], xpeer))
+    for t in (7, 1, 8, 2):
+        adv2(t)
+    tot4 = small_end(e4, q4, z4)
+    s1_ref[...] = tot4
+    gg1 = jnp.concatenate([tot4[0:1], tot4[1:2]], 1)
+    sg1 = jnp.concatenate([tot4[2:3], tot4[3:4]], 1)
+
+    def last_rows(i, _):
+        at = pl.ds(pl.multiple_of(i * 32, 32), 32)
+        nrm = (x_ref[at, :].astype(F32) - mean1) * scale1
+        ig_ref[at, :] = grecv[at, :] + gain1 * scale1 * (gacc[at, :] - sg1 * inv - nrm * gg1 * inv)
+        return 0
+
+    lax.fori_loop(0, rows // 32, last_rows, 0)
+    for c in bx:
+        c.wait_recv()
+    bs[...] = tree([bl[...], bxy[0], bxy[1], bxy[2]])
+    bz_c = [go(rcopy(bs, bz.at[i], bx_s.at[3 + i], bx_r.at[3 + i], zpeers[i])) for i in range(3)]
+    for t in (9, 3):
+        adv2(t)
+    for t in (0, 7, 1):
+        adv3(t)
+    c2.wait_recv()
+    add_into(csx, csc[xb], crx[...])
+    c3 = go(rcopy(csx.at[1 - yb], cry, cg_s.at[2], cg_r.at[2], ypeer))
+    for t in (4, 5, 6):
+        adv2(t)
+    for t in (8, 2, 9):
+        adv3(t)
+    for t in (0, 7, 1):
+        adv4(t)
+    c3.wait_recv()
+    add_into(csy, csx[yb], cry[...])
+    c4 = go(rcopy(csy.at[1 - z0], crz, cg_s.at[3], cg_r.at[3], zpeers[0]))
+    for t in (3, 4):
+        adv3(t)
+    c4.wait_recv()
+    add_into(csz, csy[z0], crz[...])
+    c5 = go(rcopy(csz.at[1 - z1b], crw, cg_s.at[4], cg_r.at[4], zpeers[1]))
+    for t in (8, 2, 9):
+        adv4(t)
+    c5.wait_recv()
+    cao[yb, z0, z1b] = (csz[z1b].astype(F32) + crw[...].astype(F32)).astype(BF16)
+    here = cao.at[yb, z0, z1b]
+    c6 = go(rcopy(here, here, cg_s.at[5], cg_r.at[5], zpeers[1]))
+    for t in (5, 6):
+        adv3(t)
+    c6.wait_recv()
+    here = cao.at[yb, z0]
+    c7 = go(rcopy(here, here, cg_s.at[6], cg_r.at[6], zpeers[0]))
+    for t in (3, 4):
+        adv4(t)
+    c7.wait_recv()
+    here = cao.at[yb]
+    c8 = go(rcopy(here, here, cg_s.at[7], cg_r.at[7], ypeer))
+    for t in (5, 6):
+        adv4(t)
+    for c in bz_c:
+        c.wait_recv()
+    bg_ref[k] = tree([bs[...], bz[0], bz[1], bz[2]])
+    bs2 = go(rcopy(bg_ref.at[k], bg_ref.at[k], bx_s.at[6], bx_r.at[6], sib))
+    mine24 = pl.ds(pl.multiple_of(24 * k, 8), 24)
+    for t in (0, 7, 1, 8, 2, 9, 3, 4, 5, 6):
+        rs5[t].wait_recv()
+        if t < 7:
+            oh_ref[:, human_cols(t, k)] = fin[t, mine24, :]
+            oh_ref[:, human_cols(t, 1 - k)] = frecv[t]
+        else:
+            wide = TILE if t < 9 else 128
+            om_ref[:, mouse_cols(t - 7, k)] = fin[t, mine24, 0:wide]
+            om_ref[:, mouse_cols(t - 7, 1 - k)] = frecv[t, :, 0:wide]
+    c8.wait_recv()
+    cg_ref[...] = cao[...].astype(F32)
+    bs2.wait_recv()
+    for c in sent:
+        if c is not g_x:
+            c.wait_send()
+
+
+def fused_on_device(
+    inputs, gain_one, shift_one, conv_weight, gain_two, shift_two, mix_weight, head_weight, head_bias, species, counts
+):
+    nseq = lax.axis_size("seq")
+    seq = lax.axis_index("seq")
+    ch = lax.axis_index("ch")
+    k = ch % 2
+    rows, width = inputs.shape
+    bins = rows * 4 * nseq
+    tracks = head_weight.shape[1]
+    hid = 96 * 4
+
+    def is_human(s, c):
+        w = window_lookup(s * rows * 4 + c * rows, bins)
+        ids = jnp.arange(species.shape[0], dtype=jnp.int32)
+        return jnp.sum(jnp.where(ids == w, species, 0)) == 0
+
+    human = is_human(seq, ch)
+    peer_seq = seq + k * (1 - 2 * (seq % 2))
+    peer_ch = ch + (1 - k) * (2 - 4 * (ch // 2))
+    flags = jnp.stack([human, is_human(peer_seq, peer_ch)]).astype(F32)
+    cw_own = jnp.concatenate([conv_weight.transpose(2, 0, 1).reshape(96, TAPS * width), mix_weight], 1)
+    zero = jnp.zeros((2, hid), F32)
+    g2 = lax.dynamic_update_slice(zero, jnp.stack([gain_two, shift_two]), (0, 96 * ch))
+    p1 = jnp.stack([gain_one, shift_one])
+    edge = HUMAN // 128 * 128
+    skip = HUMAN - edge
+    wm = jnp.pad(head_weight[:, edge:], ((0, 0), (0, 1792 - (tracks - edge))))
+
+    def human_counts(unused):
+        c = jnp.pad(counts.astype(BF16), ((0, 0), (0, 5376 - HUMAN)))
+        return jnp.stack([c[:, :2688], c[:, 2688:]])
+
+    def mouse_counts(unused):
+        c = jnp.pad(counts[:, :MOUSE].astype(BF16), ((0, 0), (skip, 1792 - skip - MOUSE)))
+        more = ((0, 0), (0, 2688 - 896))
+        return jnp.stack([jnp.pad(c[:, :896], more), jnp.pad(c[:, 896:], more)])
+
+    cs = lax.cond(human, human_counts, mouse_counts, 0)
+    hb = jnp.pad(head_bias[:HUMAN], (0, 5376 - HUMAN)).reshape(2, 2688)
+    hv = jnp.pad(jnp.ones((HUMAN,), F32), (0, 5376 - HUMAN)).reshape(2, 2688)
+    mb = jnp.pad(head_bias[HUMAN:], (skip, 1792 - skip - MOUSE)).reshape(2, 896)
+    mv = jnp.pad(jnp.ones((MOUSE,), F32), (skip, 1792 - skip - MOUSE)).reshape(2, 896)
+    more = ((0, 0), (0, 2688 - 896))
+    bv = jnp.where(human, jnp.stack([hb, hv]), jnp.stack([jnp.pad(mb, more), jnp.pad(mv, more)]))
+    bv = jnp.where(k == 0, bv[:, 0], bv[:, 1]).reshape(2, 7, TILE).transpose(1, 0, 2)
+
+    V = pltpu.VMEM
+    D = pltpu.SemaphoreType.DMA
+    vm = pl.BlockSpec(memory_space=pltpu.VMEM)
+    anywhere = pl.BlockSpec(memory_space=pl.ANY)
+    small = [(8, TILE), (2, TILE), (2, TILE), (4, TILE)]
+    scratch = [
+        V((rows, width), BF16), V((2, 16, width), BF16), V((hid, 4 * width), BF16), V((rows, hid), F32),
+        V((rows + 32, hid), F32), V((rows + 32, hid), F32),
+        V((7, 768, TILE), BF16), V((3, 768, TILE), BF16), V((768, TILE), BF16), V((7, 2 * rows, TILE), BF16),
+        V((2 * rows, width), BF16), V((width, 2 * rows), BF16), V((2 * rows, TILE), BF16),
+        V((2 * rows, width), F32), V((rows, width), F32),
+        V((7, 2, 2, 2, 2, 48, TILE), BF16), V((7, 2, 2, 2, 48, TILE), BF16), V((10, 2, 2, 2, 48, TILE), BF16),
+        V((10, 2, 2, 48, TILE), BF16), V((10, 2, 2, 48, TILE), BF16),
+        V((10, 2, 48, TILE), BF16), V((10, 2, 48, TILE), BF16), V((10, 48, TILE), BF16),
+        V((10, 48, TILE), F32), V((10, 24, TILE), F32),
+        *[V(s, F32) for s in small],
+        *[V((7, *s), F32) for s in small],
+        *[V((3, *s), F32) for s in small],
+        *[V(s, F32) for s in small],
+        V((16, TILE), F32), V((3, 16, TILE), F32), V((16, TILE), F32), V((3, 16, TILE), F32),
+        V((rows + 32, hid), F32), V((rows, hid), BF16), V((2, 16, hid), BF16), V((2, rows, hid), BF16), V((rows, hid), BF16),
+        V((2, 2, 2, 2, 2, 96, TILE), BF16), V((2, 2, 2, 2, 96, TILE), BF16), V((2, 2, 2, 2, 96, TILE), BF16),
+        V((2, 2, 2, 96, TILE), BF16), V((2, 2, 2, 96, TILE), BF16),
+        V((2, 2, 96, TILE), BF16), V((2, 2, 96, TILE), BF16),
+        V((2, 96, TILE), BF16), V((2, 96, TILE), BF16), V((96, TILE), BF16), V((2, 2, 2, 96, TILE), BF16),
+        D((4, 10)), D((4, 10)), D((2,)), D((2,)), D((6,)), D((6,)), D((10,)), D((10,)), D((10,)), D((10,)), D((10,)),
+        D((10,)), D((10,)), D((7,)), D((7,)), D((7,)),
+        D((1,)), D((1,)), D((4, 10)), D((4, 10)), D((10,)), D((10,)), D((7,)), D((7,)), D((3,)), D((3,)), D((8,)), D((8,)),
+    ]
+    S = jax.ShapeDtypeStruct
+    outs = pl.pallas_call(
+        step_kernel,
+        out_shape=[
+            S((rows, width), BF16), S((rows, width), F32), S((4, TILE), F32), S((2, hid), F32),
+            S((2, 2, 2, 96, TILE), F32), S((24, 5376), F32), S((24, 1792), F32), S((2, 16, TILE), F32),
+        ],
+        in_specs=[vm, vm, vm, vm, anywhere, anywhere, anywhere, vm, pl.BlockSpec(memory_space=pltpu.SMEM)],
+        out_specs=[vm] * 8,
+        scratch_shapes=scratch,
+        compiler_params=pltpu.CompilerParams(collective_id=0, has_side_effects=True, vmem_limit_bytes=64 * 1024 * 1024 - 128 * 1024),
+        name="step",
+    )(inputs, p1, g2, cw_own, head_weight, wm, cs, bv, flags)
+    out, ig, s1, s2, cg, oh, om, bg = outs
+    cg = cg.reshape(4, 2, 96, TILE)
+    conv_grad = cg[:3].transpose(0, 1, 3, 2).reshape(TAPS, width, 96)
+    mix_grad = cg[3].transpose(1, 0, 2).reshape(96, width)
+    s2 = lax.dynamic_slice(s2, (0, 96 * ch), (2, 96))
+    head_grad = jnp.concatenate([oh[:, :HUMAN], om[:, skip:skip + MOUSE]], 1)
+    bias_h = bg[:, :7].reshape(2, 2688).reshape(-1)[:HUMAN]
+    bias_m = bg[:, 8:11].reshape(2, 3 * TILE)[:, :896].reshape(-1)[skip:skip + MOUSE]
+    return (
+        out, ig, s1[:2].reshape(-1), s1[2:].reshape(-1), conv_grad, s2[0], s2[1], mix_grad, head_grad,
+        jnp.concatenate([bias_h, bias_m]),
+    )
+
+
 def solution(mesh):
     in_specs = (
         P(("seq", "ch"), None),
@@ -311,6 +941,8 @@
         P(("seq", "ch"), None),
         P(),
     )
+    fits = mesh.shape["seq"] == 8 and mesh.shape["ch"] == 4
+    body = fused_on_device if fits else on_device
     return jax.shard_map(
-        on_device, mesh=mesh, in_specs=in_specs, out_specs=out_specs, check_vma=False
-    )
+        body, mesh=mesh, in_specs=in_specs, out_specs=out_specs, check_vma=False
+    )

time: 632 us -> 187 us (0.30)
  waiting for transfers between devices: 379 us -> 0 us
  Pallas kernels: 0 us -> 155 us
  blocking collectives: 123 us -> 0 us
  matrix products: 34.1 us -> 0 us
  local copies, waits for them, and re-layouts: 43.6 us -> 17 us
  other arithmetic: 28.4 us -> 11.4 us
  between operations: 15.2 us -> 2.24 us
  starting transfers between devices: 7.34 us -> 0 us
    unnamed x8 -> x0, waiting for transfers between devices: 229 us -> none
    pallas_call x0 -> x1, Pallas kernels: none -> 155 us  [fused_on_device(): pl.pallas_call(step_kernel, out_shape=[S((rows, width), BF16), S((rows, w...]
    psum x4 -> x0, blocking collectives: 123 us -> none  [the longest x1 42.1 us: on_device(): lax.psum((jnp.sum(input_f, 0), jnp.sum(input_f * input_f, 0)), ('seq', 'c...]
    all_gather x3 -> x0, waiting for transfers between devices: 111 us -> none  [the longest x1 71.8 us: on_device(): grad_out = back_piece(lax.all_gather(head_weight, 'ch', axis=0, tiled=True))]
    dot_general x15 -> x0, matrix products: 34.1 us -> none  [the longest x1 6.56 us: human_back(): lax.dot_general(grad_human, piece[:, :HUMAN], contract_cols, preferred_el...]
    psum x1 -> x0, waiting for transfers between devices: 24.2 us -> none  [on_device(): conv_weight_grad, mix_weight_grad = lax.psum((conv_part, mix_part), 'seq')]
    cond x1, local copies, waits for them, and re-layouts: 21.4 us -> 2.95 us  [fused_on_device(): cs = lax.cond(human, human_counts, mouse_counts, 0)]
    convert_element_type x7 -> x2, other arithmetic: 19 us -> 3.57 us  [the longest x1 2.99 us: human_counts(): c = jnp.pad(counts.astype(BF16), ((0, 0), (0, 5376 - HUMAN)))]
  transfers between devices with their start and end apart: 11 -> 0, of which waited for: 8 -> 0; matrix products, arithmetic and copies ran while one was open for 11% -> 0% of each run, Pallas kernels for 0% -> 0%
where the time goes in v1:
time: 187 us; the launch traced here: 186 us
  Pallas kernels  155 us (83%)
  local copies, waits for them, and re-layouts  17 us (9%)
  other arithmetic  11.4 us (6%)
  between operations  2.24 us (1%)
    pallas_call x1, Pallas kernels, fused_on_device(): pl.pallas_call(step_kernel, out_shape=[S((rows, width), BF16), S((rows, w...  155 us

profile of v1, /device:TPU:0, one launch (start us, length us, event | category | flops | bytes accessed | tf_op | source)
XLA Modules:
  0.0 185.9 jit_solution(1924310159361948746)
XLA Ops:
  0.8 1.3 fusion.2
  3.4 0.6 add_convert_fusion.flag_ref
  4.0 0.7 pad_maximum_fusion.6
  4.6 0.7 stack.57
  5.3 0.7 stack.58
  6.0 0.6 pad_maximum_fusion.5.p1_ref
  6.7 0.8 slice.74
  7.8 0.8 slice_select_fusion
  8.7 0.6 slice_select_fusion.1
  9.3 1.1 copy.39
  10.4 0.9 pad_maximum_fusion.3.cwo_ref
  11.3 0.9 pad.42.wm_ref
  12.2 6.4 %conditional.1 = (bf16[2,256,2688]{2,1,0:T(8,128)(2,1)}) conditional(s32[]{:T(128)} %convert_element_type.28, s32[256,5313]{0,1:T(8,128)} %param.23, s32[256,5313]{0,1:T(8,128)} %param.23), branch_computations={%region_1.2_spmd, %region_2.3_spmd} | conditional | flops 2736384 | bytes 26023432 | solution.py:853
  12.2 3.0 %convert_element_type.25 = bf16[256,5313]{0,1:T(8,128)(2,1)S(1)} convert(s32[256,5313]{0,1:T(8,128)} %param.1) | non-fusion elementwise | flops 1360128 | bytes 8160768 | tf_op jit(solution)/shard_map/cond/branch_1_fun/convert_element_type | solution.py:845
  15.2 0.2 slice_bitcast_fusion
  15.4 0.3 pad_maximum_fusion.1
  15.6 2.9 %copy.38 = bf16[2,256,2688]{2,1,0:T(8,128)(2,1)} copy(bf16[2,256,2688]{1,2,0:T(8,128)(2,1)S(1)} %pad_maximum_fusion.1) | data formatting | bytes 5505024 | tf_op jit(solution)/shard_map/cond | solution.py:853
  18.6 155.2 %step.1 = (bf16[256,768]{1,0:T(8,128)(2,1)}, f32[256,768]{1,0:T(8,128)}, f32[4,384]{1,0:T(4,128)}, f32[2,384]{1,0:T(2,128)}, f32[2,2,2,96,384]{4,3,2,1,0:T(8,128...) custom-call(bf16[256,768]{1,0:T(8,128)(2,1)} %x_ref.1, f32[2,768]{1,0:T(2,128)} %pad_maximum_fusion.5.p1_ref, ...), custom_call_target="tpu_custom_call" | custom-call | tf_op jit(solution)/shard_map/step/pallas_call | solution.py:892
  173.8 0.8 constant_dynamic-slice_fusion
  174.6 0.5 slice_bitcast_fusion.4
  175.1 0.8 fusion.3
  175.9 0.6 reshape.73
  176.5 0.6 reshape.72
  177.1 0.7 slice_bitcast_fusion.3
  177.8 0.7 slice.85
  178.7 0.7 pad_maximum_fusion.4
  179.4 1.0 slice.84
  180.4 2.0 %pad_maximum_fusion.2 = f32[24,6956]{1,0:T(8,128)} fusion(f32[24,1643]{1,0:T(8,128)S(1)} %slice.84, f32[24,5313]{1,0:T(8,128)} %bitcast.42), kind=kLoop, calls=%fused_computation.11 | loop fusion | flops 166944 | bytes 1335552 | tf_op jit(solution)/shard_map/concatenate | solution.py:909
  182.5 1.0 copy.40
  183.5 0.7 copy.41
  184.2 0.7 copy.48
  185.0 0.9 copy.49
  (35 shorter events, 0.7 us)
Async XLA Ops:
  0.6 9.8 %copy-start.3 = (bf16[96,768]{1,0:T(8,128)(2,1)S(1)}, bf16[96,768]{1,0:T(8,128)(2,1)}, u32[]{:S(2)}) copy-start(bf16[96,768]{1,0:T(8,128)(2,1)} %param.19) | copy-start | bytes 442372
  6.7 4.6 %copy-start.4 = (f32[2,384]{1,0:T(2,128)}, f32[2,384]{1,0:T(2,128)S(1)}, u32[]{:S(2)}) copy-start(f32[2,384]{1,0:T(2,128)S(1)} %dynamic_update_slice.3.g2_ref) | copy-start | bytes 9220
  9.3 2.0 %slice-start = ((bf16[192,6956]{1,0:T(8,128)(2,1)}), bf16[192,1708]{1,0:T(8,128)(2,1)S(1)}, s32[]{:S(2)}) async-start(bf16[192,6956]{1,0:T(8,128)(2,1)} %w_ref.1), calls=%async_computation | async-start | bytes 1376256 | tf_op jit(solution)/shard_map/slice | solution.py:842
  173.8 8.7 %copy-start = (f32[2,2,2,96,384]{4,3,2,1,0:T(8,128)S(1)}, f32[2,2,2,96,384]{4,3,2,1,0:T(8,128)}, u32[]{:S(2)}) copy-start(f32[2,2,2,96,384]{4,3,2,1,0:T(8,128)} %get-tuple-element.26) | copy-start | bytes 3538948
  182.4 1.8 copy-start.2
  182.5 2.5 %copy-start.1 = (f32[256,768]{1,0:T(8,128)S(1)}, f32[256,768]{1,0:T(8,128)}, u32[]{:S(2)}) copy-start(f32[256,768]{1,0:T(8,128)} %get-tuple-element.57) | copy-start | bytes 2359300
